TPU v7x, 32 devices: a whole 2x2x4 slice. The times are simulated.
32 devices in a mesh: row: 16 (over z, y, x), col: 2 (over core).
Axes of the slice: x: 2, y: 2, z: 4, core: 2. Of those that a mesh axis runs over, the one named last changes fastest.
Arguments:
- matrix: float32 [3072, 3072], P('row', 'col'), may hold values from -2 to 2, as said below
- diagonal: float32 [3072], P(('row', 'col')), may hold values from 1 to 6
- start: float32 [3072], P(('row', 'col')), may hold values from -6 to 6
Outputs:
- basis: float32 [4, 3072], P(None, ('row', 'col'))
- coefficients: float32 [2, 3], replicated
Inputs may be any that keep to these rules, and one draw needn't show every extreme that they name: matrix is exactly symmetric, its entries of order one over the square root of 3072.
All inputs are finite; a program needn't handle non-finite values.
Results may differ from a plain program's by a relative error of at most 0.0003.
Values sent between devices are 32-bit elements.
A program may use at most 64 MiB of HBM per device.

v0:
```python
import math

import jax
import jax.numpy as jnp
from jax import lax
from jax.sharding import PartitionSpec as P

ITERS = 3


def per_device(matrix, diagonal, start):
    rows_total = lax.axis_size("row")
    cols_total = lax.axis_size("col")
    tile_len = start.shape[0]
    full_dim = tile_len * rows_total * cols_total
    col_len = matrix.shape[1]
    col_idx = lax.axis_index("col")

    def apply_matrix(vector):
        gathered = lax.all_gather(vector, ("row", "col"), axis=0, tiled=True)
        column = lax.dynamic_slice_in_dim(gathered, col_idx * col_len, col_len, 0)
        partial_value = jnp.dot(
            matrix, column, precision=lax.Precision.HIGHEST, preferred_element_type=jnp.float32
        )
        return (
            lax.psum_scatter(partial_value, "col", scatter_dimension=0, tiled=True)
            + diagonal * vector
        )

    start_sq = lax.psum(jnp.sum(start * start), ("row", "col"))
    current = start / jnp.sqrt(start_sq)
    basis_rows = jnp.zeros((ITERS + 1, tile_len), jnp.float32).at[0].set(current)
    alpha_list = []
    beta_list = []
    for iteration in range(ITERS):
        image = apply_matrix(current)
        local_intersect = jnp.dot(
            basis_rows, image, precision=lax.Precision.HIGHEST, preferred_element_type=jnp.float32
        )
        intersect, total_sq = lax.psum((local_intersect, jnp.sum(image * image)), ("row", "col"))
        image = image - jnp.dot(
            intersect,
            basis_rows,
            precision=lax.Precision.HIGHEST,
            preferred_element_type=jnp.float32,
        )
        squared = total_sq - jnp.sum(intersect * intersect)
        beta_value = jnp.sqrt(squared)
        current = image / beta_value
        basis_rows = basis_rows.at[iteration + 1].set(current)
        alpha_list.append(intersect[iteration])
        beta_list.append(beta_value)
    coefficients = jnp.stack([jnp.stack(alpha_list), jnp.stack(beta_list)])
    return (basis_rows * jnp.float32(math.sqrt(full_dim)), coefficients)


def solution(mesh):
    in_specs = (P("row", "col"), P(("row", "col")), P(("row", "col")))
    out_specs = (P(None, ("row", "col")), P())
    return jax.shard_map(
        per_device, mesh=mesh, in_specs=in_specs, out_specs=out_specs, check_vma=False
    )
```

profile of v0, /device:TPU:0, one launch (start us, length us, event | category | flops | bytes accessed | tf_op | source)
XLA Modules:
  0.0 311.8 jit_solution(1088901283109628407)
XLA Ops:
  0.6 0.0 copy-start
  0.6 0.0 copy-start.2
  0.7 0.0 copy-start.1
  0.7 1.4 multiply_reduce_fusion.6
  2.0 42.1 %psum.49 = f32[]{:T(128)} all-reduce(f32[]{:T(128)} %multiply_reduce_fusion.6), channel_id=1, replica_groups=mesh['row'=16,'col'=2] {'row','col'}, use_global_device_ids=true, to_apply=%region_1.0 | all-reduce | flops 1 | bytes 8 | tf_op jit(solution)/shard_map/psum | solution.py:30
  44.9 0.8 fusion.17
  45.6 40.5 %all-reduce.1 = f32[3072]{0:T(1024)S(1)} all-reduce(f32[3072]{0:T(1024)S(1)} %get-tuple-element.62), channel_id=1, replica_groups=mesh['row'=16,'col'=2] {'row','col'}, use_global_device_ids=true, to_apply=%add.1 | all-reduce | flops 3072 | bytes 24576
  86.1 0.1 dynamic_slice.9
  86.2 0.0 copy-done
  86.2 1.0 fusion.18
  87.2 2.5 all-reduce.4
  89.7 0.0 copy-done.2
  89.7 0.6 dynamic-slice.31
  90.9 0.0 copy-done.1
  91.0 0.7 multiply_reduce_fusion.5
  91.6 0.1 convolution_bitcast_fusion.5
  91.8 39.9 %all-reduce.9 = (f32[4]{0:T(128)S(1)}, f32[]{:T(128)}) all-reduce(f32[4]{0:T(128)S(1)} %convolution_bitcast_fusion.5, f32[]{:T(128)} %get-tuple-element.60), channel_id=1, replica_groups=mesh['row'=16,'col'=2] {'row','col'}, use_global_device_ids=true, to_apply=%region_3.0 | all-reduce | flops 5 | bytes 40 | tf_op jit(solution)/shard_map/psum | solution.py:40
  131.7 0.6 multiply_reduce_fusion.4
  133.6 0.1 fusion.1
  133.8 0.3 dynamic-update-slice.13
  134.0 40.5 %all-reduce.2 = f32[3072]{0:T(1024)S(1)} all-reduce(f32[3072]{0:T(1024)S(1)} %dynamic-update-slice.13), channel_id=1, replica_groups=mesh['row'=16,'col'=2] {'row','col'}, use_global_device_ids=true, to_apply=%add.2 | all-reduce | flops 3072 | bytes 24576
  174.6 0.1 dynamic_slice.10
  174.6 1.0 fusion.19
  175.7 2.5 all-reduce.5
  178.1 0.7 multiply_reduce_fusion.3
  178.8 0.1 convolution_bitcast_fusion.3
  179.0 39.9 %all-reduce.8 = (f32[4]{0:T(128)S(1)}, f32[]{:T(128)}) all-reduce(f32[4]{0:T(128)S(1)} %convolution_bitcast_fusion.3, f32[]{:T(128)} %get-tuple-element.58), channel_id=1, replica_groups=mesh['row'=16,'col'=2] {'row','col'}, use_global_device_ids=true, to_apply=%region_8.0 | all-reduce | flops 5 | bytes 40 | tf_op jit(solution)/shard_map/psum | solution.py:40
  218.9 0.7 multiply_reduce_fusion.2
  220.9 0.1 fusion.3
  221.1 0.3 dynamic-update-slice.14
  221.3 40.6 %all-reduce.3 = f32[3072]{0:T(1024)S(1)} all-reduce(f32[3072]{0:T(1024)S(1)} %dynamic-update-slice.14), channel_id=1, replica_groups=mesh['row'=16,'col'=2] {'row','col'}, use_global_device_ids=true, to_apply=%add.3 | all-reduce | flops 3072 | bytes 24576
  261.9 0.1 dynamic_slice.11
  262.0 1.0 fusion.20
  263.0 2.5 all-reduce.6
  265.4 0.7 multiply_reduce_fusion.1
  266.1 0.1 convolution_bitcast_fusion.1
  266.3 39.8 %all-reduce.7 = (f32[4]{0:T(128)S(1)}, f32[]{:T(128)}) all-reduce(f32[4]{0:T(128)S(1)} %convolution_bitcast_fusion.1, f32[]{:T(128)} %get-tuple-element.56), channel_id=1, replica_groups=mesh['row'=16,'col'=2] {'row','col'}, use_global_device_ids=true, to_apply=%region_13.0 | all-reduce | flops 5 | bytes 40 | tf_op jit(solution)/shard_map/psum | solution.py:40
  306.1 0.6 multiply_reduce_fusion
  308.0 0.6 slice.70
  308.6 0.6 slice.69
  309.2 1.3 maximum_bitcast_fusion
  310.4 0.6 pad_maximum_fusion
  311.0 0.1 fusion.6
  311.2 0.6 broadcast_multiply_fusion
  (10 shorter events, 0.1 us)
Async XLA Ops:
  0.6 85.6 %copy-start = (f32[192,1536]{1,0:T(8,128)S(1)}, f32[192,1536]{1,0:T(8,128)}, u32[]{:S(2)}) copy-start(f32[192,1536]{1,0:T(8,128)} %param.11) | copy-start | bytes 3538948
  0.6 89.1 %copy-start.2 = (u32[32]{0:T(128)S(1)}, u32[32]{0:T(128)}, u32[]{:S(2)}) copy-start(u32[32]{0:T(128)} %constant.141) | copy-start | bytes 388
  0.7 90.3 %copy-start.1 = (f32[96]{0:T(128)S(1)}, f32[96]{0:T(128)}, u32[]{:S(2)}) copy-start(f32[96]{0:T(128)} %param.12) | copy-start | bytes 1156
where the time goes:
time: 313 us; the launch traced here: 312 us
  blocking collectives  291 us (93%)
  other arithmetic  8.45 us (3%)
  between operations  6.07 us (2%)
  matrix products  3.81 us (1%)
    unnamed x6, blocking collectives  129 us
    psum x3, blocking collectives, per_device(): lax.psum((local_intersect, jnp.sum(image * image)), ('row', 'col'))  120 us
    psum x1, blocking collectives, per_device(): start_sq = lax.psum(jnp.sum(start * start), ('row', 'col'))  42.1 us

commit v1 on v0

v1 whole, which is shorter than its diff:
```python
import functools
import math

import jax
import jax.numpy as jnp
from jax import lax
from jax.experimental import pallas as pl
from jax.experimental.pallas import tpu as pltpu
from jax.sharding import PartitionSpec as P

ITERS = 3
LANES = 128
MESH = pl.DeviceIdType.MESH


class Plan:
    def __init__(self, rows, cols, block, width, chunk):
        self.rows, self.cols, self.block, self.width, self.chunk = rows, cols, block, width, chunk
        self.devices = rows * cols
        self.group = LANES // math.gcd(block, LANES)
        self.tiles = self.group * block // LANES
        self.groups = rows // self.group
        self.bases = [p * block // LANES for p in range(self.group)]
        self.heights = [-(-(p * block % LANES + block) // LANES) for p in range(self.group)]
        self.height = max(self.heights)
        self.col_groups = width // (self.group * block)
        assert rows % self.group == 0 and width % (self.group * block) == 0
        assert chunk * cols == block


def kernel(plan, m_hbm, d_ref, s_ref, basis_ref, coef_ref, m_ref, send, recv, full, m_sem, send_sem, recv_sem):
    n, height, tiles, groups = plan.devices, plan.height, plan.tiles, plan.groups
    row, col = lax.axis_index("row"), lax.axis_index("col")
    me = row * plan.cols + col
    part = lax.rem(row, plan.group)
    offset = lax.rem(part * plan.block, LANES)
    base = (part * plan.block) // LANES
    my_group = row // plan.group

    m_copy = pltpu.make_async_copy(
        m_hbm, m_ref.at[pl.ds(pl.multiple_of(offset, 8), plan.block), :], m_sem
    )
    m_copy.start()

    barrier = pltpu.get_barrier_semaphore()
    peers = []
    for step in range(1, n):
        other = lax.rem(me + step, n)
        peers.append((other // plan.cols, lax.rem(other, plan.cols)))
    for peer in peers:
        pl.semaphore_signal(barrier, inc=1, device_id=peer, device_id_type=MESH)

    def spread(chunk):
        wide = jnp.concatenate(
            [chunk, jnp.zeros((1, height * LANES - plan.chunk), jnp.float32)], axis=1
        )
        return pltpu.roll(wide, offset + col * plan.chunk, 1)

    diagonal = spread(d_ref[...])
    first = spread(s_ref[...])
    lane = lax.broadcasted_iota(jnp.int32, (1, height * LANES), 1)
    inside = (lane >= offset) & (lane < offset + plan.block)

    def post(phase, value):
        for h in range(height):
            tile = value[:, h * LANES : (h + 1) * LANES]
            send[phase, pl.ds(h, 1), :] = tile
            recv[phase, me, pl.ds(h, 1), :] = tile

    def start(phase):
        for peer in peers:
            pltpu.make_async_remote_copy(
                src_ref=send.at[phase],
                dst_ref=recv.at[phase, me],
                send_sem=send_sem.at[phase],
                recv_sem=recv_sem.at[phase],
                device_id=peer,
                device_id_type=MESH,
            ).start()

    def bulk(sem):
        def wait(phase):
            region = recv.at[phase, pl.ds(0, n - 1)]
            pltpu.make_async_copy(region, region, sem.at[phase]).wait()

        return wait

    wait_recv, wait_send = bulk(recv_sem), bulk(send_sem)

    def collect(phase):
        out = [None] * tiles
        for p in range(plan.group):
            for h in range(plan.heights[p]):
                for c in range(plan.cols):
                    value = recv[
                        phase, pl.ds(p * plan.cols + c, groups, stride=plan.group * plan.cols), h, :
                    ]
                    k = plan.bases[p] + h
                    out[k] = value if out[k] is None else out[k] + value
        return out

    def total(values):
        acc = values[0]
        for value in values[1:]:
            acc = acc + value
        return jnp.sum(acc, axis=(0, 1), keepdims=True)

    def keep(index, values):
        for k in range(tiles):
            full[index, k] = values[k]

    def product(index):
        begin = col * plan.col_groups
        partial = []
        for h in range(height):
            acc = None
            for g in range(plan.col_groups):
                for k in range(tiles):
                    t = g * tiles + k
                    v = full[index, k, pl.ds(begin + g, 1), :]
                    term = m_ref[pl.ds(h * LANES, LANES), pl.ds(t * LANES, LANES)] * v
                    acc = term if acc is None else acc + term
            partial.append(jnp.sum(acc.T, axis=0, keepdims=True))
        value = jnp.where(inside, jnp.concatenate(partial, axis=1), 0.0)
        mine = jnp.concatenate(
            [
                full[index, jnp.minimum(base + h, tiles - 1), pl.ds(my_group, 1), :]
                for h in range(height)
            ],
            axis=1,
        )
        return value + diagonal * mine

    scale = math.sqrt(plan.rows * plan.block)
    place = me * plan.chunk
    t0 = place // LANES
    t1 = jnp.minimum(t0 + 1, tiles * groups - 1)
    shift = lax.rem(2 * LANES - lax.rem(place, LANES), 2 * LANES)

    def emit(index):
        pair = [full[index, lax.rem(t, tiles), pl.ds(t // tiles, 1), :] for t in (t0, t1)]
        value = pltpu.roll(jnp.concatenate(pair, axis=1), shift, 1)
        basis_ref[pl.ds(index, 1), :] = value[:, : plan.chunk] * scale

    post(0, first)
    pl.semaphore_wait(barrier, n - 1)
    start(0)
    wait_recv(0)
    values = collect(0)
    inverse = 1.0 / jnp.sqrt(total([v * v for v in values]))
    rows_q = [[v * inverse for v in values]]
    keep(0, rows_q[0])
    alphas, betas = [], []
    m_copy.wait()
    for k in range(ITERS):
        post(k + 1, product(k))
        start(k + 1)
        emit(k)
        wait_recv(k + 1)
        values = collect(k + 1)
        h = [total([a * b for a, b in zip(values, q)]) for q in rows_q]
        for value, q in zip(h, rows_q):
            values = [a - value * b for a, b in zip(values, q)]
        beta = jnp.sqrt(total([a * a for a in values]))
        inverse = 1.0 / beta
        rows_q.append([a * inverse for a in values])
        keep(k + 1, rows_q[-1])
        alphas.append(h[k])
        betas.append(beta)
    emit(ITERS)
    coef_ref[...] = jnp.concatenate(
        [jnp.concatenate(alphas, axis=1), jnp.concatenate(betas, axis=1)], axis=0
    )
    for phase in range(ITERS + 1):
        wait_send(phase)


def per_device(plan, matrix, diagonal, start):
    chunk = plan.chunk
    n, phases = plan.devices, ITERS + 1
    vmem = pl.BlockSpec(memory_space=pltpu.VMEM)
    return pl.pallas_call(
        functools.partial(kernel, plan),
        out_shape=(
            jax.ShapeDtypeStruct((phases, chunk), jnp.float32),
            jax.ShapeDtypeStruct((2, ITERS), jnp.float32),
        ),
        in_specs=[pl.BlockSpec(memory_space=pl.ANY), vmem, vmem],
        out_specs=(vmem, vmem),
        scratch_shapes=[
            pltpu.VMEM((plan.height * LANES, plan.width), jnp.float32),
            pltpu.VMEM((phases, plan.height, LANES), jnp.float32),
            pltpu.VMEM((phases, n, plan.height, LANES), jnp.float32),
            pltpu.VMEM((phases, plan.tiles, plan.groups, LANES), jnp.float32),
            pltpu.SemaphoreType.DMA,
            pltpu.SemaphoreType.DMA((phases,)),
            pltpu.SemaphoreType.DMA((phases,)),
        ],
        compiler_params=pltpu.CompilerParams(collective_id=0, has_side_effects=True),
    )(matrix, diagonal.reshape(1, chunk), start.reshape(1, chunk))


def solution(mesh):
    rows, cols = mesh.shape["row"], mesh.shape["col"]

    def run(matrix, diagonal, start):
        plan = Plan(rows, cols, matrix.shape[0], matrix.shape[1], start.shape[0])
        return per_device(plan, matrix, diagonal, start)

    in_specs = (P("row", "col"), P(("row", "col")), P(("row", "col")))
    out_specs = (P(None, ("row", "col")), P())
    return jax.shard_map(run, mesh=mesh, in_specs=in_specs, out_specs=out_specs, check_vma=False)
```

time: 313 us -> 31.4 us (0.10)
  blocking collectives: 291 us -> 0 us
  Pallas kernels: 0 us -> 28.1 us
  other arithmetic: 8.45 us -> 0 us
  between operations: 6.07 us -> 0.64 us
  matrix products: 3.81 us -> 0 us
    psum x4 -> x0, blocking collectives: 162 us -> none  [the longest x3 120 us: per_device(): lax.psum((local_intersect, jnp.sum(image * image)), ('row', 'col'))]
    unnamed x6 -> x0, blocking collectives: 129 us -> none
    pallas_call x0 -> x1, Pallas kernels: none -> 28.1 us  [per_device(): pl.pallas_call(functools.partial(kernel, plan), out_shape=(jax.ShapeDtype...]
    reduce_sum x7 -> x0, other arithmetic: 5.24 us -> none  [the longest x3 2.02 us: per_device(): jnp.sum(image * image)]
    dot_general x9 -> x0, matrix products: 3.81 us -> none  [the longest x3 3.04 us: apply_matrix(): jnp.dot(matrix, column, precision=lax.Precision.HIGHEST, preferred_elemen...]
where the time goes in v1:
time: 31.4 us; the launch traced here: 31.2 us
  Pallas kernels  28.1 us (89%)
  local copies, waits for them, and re-layouts  2.46 us (8%)
  between operations  0.64 us (2%)
    pallas_call x1, Pallas kernels, per_device(): pl.pallas_call(functools.partial(kernel, plan), out_shape=(jax.ShapeDtype...  28.1 us
    unnamed x2, local copies, waits for them, and re-layouts  2.46 us

profile of v1, /device:TPU:0, one launch (start us, length us, event | category | flops | bytes accessed | tf_op | source)
XLA Modules:
  0.0 31.2 jit_solution(16881134168690062747)
XLA Ops:
  0.6 28.1 %shard_map.50 = (f32[4,96]{1,0:T(4,128)}, f32[2,3]{1,0:T(2,128)}) custom-call(f32[192,1536]{1,0:T(8,128)} %m_hbm.1, f32[1,96]{1,0:T(1,128)} %bitcast.2, f32[1,96]{1,0:T(1,128)} %bitcast.3), custom_call_target="tpu_custom_call" | custom-call | tf_op jit(solution)/shard_map/pallas_call | solution.py:182
  28.8 1.2 %copy.7 = f32[4,96]{1,0:T(4,128)} copy(f32[4,96]{1,0:T(4,128)} %get-tuple-element.4) | data formatting | bytes 3072
  30.0 1.2 %copy.8 = f32[2,3]{1,0:T(2,128)} copy(f32[2,3]{1,0:T(2,128)} %get-tuple-element.5) | data formatting | bytes 48

commit v2 on v1

v2 whole, which is shorter than its diff:
```python
import functools
import math

import jax
import jax.numpy as jnp
from jax import lax
from jax.experimental import pallas as pl
from jax.experimental.pallas import tpu as pltpu
from jax.sharding import PartitionSpec as P

ITERS = 3
LANES = 128
MESH = pl.DeviceIdType.MESH


class Plan:
    def __init__(self, rows, cols, block, width, chunk):
        self.rows, self.cols, self.block, self.width, self.chunk = rows, cols, block, width, chunk
        self.devices = rows * cols
        self.group = LANES // math.gcd(block, LANES)
        self.tiles = self.group * block // LANES
        self.groups = rows // self.group
        self.bases = [p * block // LANES for p in range(self.group)]
        self.heights = [-(-(p * block % LANES + block) // LANES) for p in range(self.group)]
        self.height = max(self.heights)
        self.col_groups = width // (self.group * block)
        assert rows % self.group == 0 and width % (self.group * block) == 0
        assert chunk * cols == block and cols == 2


def kernel(
    plan, m_hbm, d_hbm, s_hbm, basis_ref, coef_ref,
    m_ref, d_ref, s_ref, d_send, d_all, send, first, recv, full, basis,
    m_sem, d_sem, s_sem, m_over, d_over, send_sem, recv_sem,
):
    n, rows, cols = plan.devices, plan.rows, plan.cols
    height, tiles, groups = plan.height, plan.tiles, plan.groups
    row, col = lax.axis_index("row"), lax.axis_index("col")
    me = row * cols + col
    lead = cols - 1
    part = lax.rem(row, plan.group)
    offset = lax.rem(part * plan.block, LANES)
    base = (part * plan.block) // LANES
    my_group = row // plan.group
    wide = height * LANES

    peers = [partner(me, step, n) for step in range(n - 1, 0, -1)]
    peers = [(other // cols, lax.rem(other, cols)) for other in peers]
    barrier = pltpu.get_barrier_semaphore()
    for peer in peers:
        pl.semaphore_signal(barrier, inc=1, device_id=peer, device_id_type=MESH)

    def spread(chunk):
        padded = jnp.concatenate([chunk, jnp.zeros((1, wide - plan.chunk), jnp.float32)], axis=1)
        return pltpu.roll(padded, offset + col * plan.chunk, 1)

    def put(ref, index, value):
        for h in range(height):
            ref[index, pl.ds(h, 1), :] = value[:, h * LANES : (h + 1) * LANES]

    def remote(src, dst, ssem, rsem, peer):
        return pltpu.make_async_remote_copy(
            src_ref=src, dst_ref=dst, send_sem=ssem, recv_sem=rsem, device_id=peer, device_id_type=MESH
        )

    def bulk(count, sem):
        region = first.at[pl.ds(0, count)]
        pltpu.make_async_copy(region, region, sem).wait()

    def gathered(load, count):
        out = [None] * tiles
        for p in range(plan.group):
            for h in range(plan.heights[p]):
                for c in range(count):
                    value = load(p * count + c, plan.group * count, h)
                    k = plan.bases[p] + h
                    out[k] = value if out[k] is None else out[k] + value
        return out

    def total(values):
        acc = values[0]
        for value in values[1:]:
            acc = acc + value
        return jnp.sum(acc, axis=(0, 1), keepdims=True)

    def dot(a, b):
        return total([x * y for x, y in zip(a, b)])

    def store(ref, index, values):
        for k in range(tiles):
            ref[index, k] = values[k]

    def product(index):
        partial = []
        for low in range(0, plan.block, LANES):
            size = min(LANES, plan.block - low)
            acc = None
            for t in range(cols * plan.width // LANES):
                v = full[index, t % tiles, pl.ds(t // tiles, 1), :]
                term = m_ref[pl.ds(low, size), pl.ds(t * LANES, LANES)] * v
                acc = term if acc is None else acc + term
            partial.append(jnp.sum(acc.T, axis=0, keepdims=True))
        if wide > plan.block:
            partial.append(jnp.zeros((1, wide - plan.block), jnp.float32))
        value = pltpu.roll(jnp.concatenate(partial, axis=1), offset, 1)
        mine = jnp.concatenate(
            [
                full[index, jnp.minimum(base + h, tiles - 1), pl.ds(my_group, 1), :]
                for h in range(height)
            ],
            axis=1,
        )
        diagonal = jnp.concatenate(
            [sum(d_all[c, pl.ds(h, 1), :] for c in range(cols)) for h in range(height)], axis=1
        )
        return value + diagonal * mine

    scale = math.sqrt(rows * plan.block)
    place = me * plan.chunk
    t0 = place // LANES
    t1 = jnp.minimum(t0 + 1, tiles * groups - 1)
    shift = lax.rem(2 * LANES - lax.rem(place, LANES), 2 * LANES)

    def emit(index):
        pair = [basis[index, lax.rem(t, tiles), pl.ds(t // tiles, 1), :] for t in (t0, t1)]
        value = pltpu.roll(jnp.concatenate(pair, axis=1), shift, 1)
        basis_ref[pl.ds(index, 1), :] = value[:, : plan.chunk] * scale

    def body(leading):
        half = m_ref.at[:, pl.ds(pl.multiple_of(col * plan.width, LANES), plan.width)]
        copies = [
            pltpu.make_async_copy(s_hbm, s_ref, s_sem),
            pltpu.make_async_copy(d_hbm, d_ref, d_sem),
            pltpu.make_async_copy(m_hbm, half, m_sem),
        ]
        for copy in copies:
            copy.start()
        copies[0].wait()
        value = spread(s_ref[...])
        put(send, 0, value)
        put(first, me, value)
        copies[1].wait()
        put(d_all if leading else d_send, lead if leading else 0, spread(d_ref[...]))
        pl.semaphore_wait(barrier, n - 1)
        for peer in peers:
            remote(send.at[0], first.at[me], send_sem.at[0], recv_sem.at[0], peer).start()
        copies[2].wait()
        over = (
            remote(d_send.at[0], d_all.at[col], d_over.at[0], d_over.at[1], (row, lead)),
            remote(half, half, m_over.at[0], m_over.at[1], (row, lead)),
        )
        if not leading:
            for copy in over:
                copy.start()
        bulk(n - 1, recv_sem.at[0])
        raw = gathered(lambda at, stride, h: first[pl.ds(at, groups, stride=stride), h, :], cols)
        if leading:
            for c in range(lead):
                other = m_ref.at[:, pl.ds(c * plan.width, plan.width)]
                remote(other, other, m_over.at[0], m_over.at[1], (row, c)).wait_recv()
                remote(d_send.at[0], d_all.at[c], d_over.at[0], d_over.at[1], (row, c)).wait_recv()
        q, images, alphas, betas = [], [], [], []
        for k in range(ITERS + 1):
            store(full, k, raw)
            image = product(k) if leading and k < ITERS else None
            h = [dot(raw, other) for other in q]
            rest = raw
            for value, other in zip(h, q):
                rest = [a - value * b for a, b in zip(rest, other)]
            beta = jnp.sqrt(dot(rest, rest))
            inverse = 1.0 / beta
            if k:
                alphas.append(h[k - 1])
                betas.append(beta)
            if image is not None:
                for value, other in zip(h, images):
                    image = image - value * other
                image = image * inverse
                images.append(image)
                put(send, k + 1, image)
                put(recv, k * rows + row, image)
                for peer in peers:
                    remote(
                        send.at[k + 1],
                        recv.at[k * rows + row],
                        send_sem.at[k + 1],
                        recv_sem.at[k + 1],
                        peer,
                    ).start()
            q.append([a * inverse for a in rest])
            store(basis, k, q[-1])
            emit(k)
            if k < ITERS:
                bulk(rows - 1 if leading else rows, recv_sem.at[k + 1])
                raw = gathered(
                    lambda at, stride, h: recv[pl.ds(k * rows + at, groups, stride=stride), h, :], 1
                )
        coef_ref[...] = jnp.concatenate(
            [jnp.concatenate(alphas, axis=1), jnp.concatenate(betas, axis=1)], axis=0
        )
        bulk(n - 1, send_sem.at[0])
        if leading:
            for k in range(ITERS):
                bulk(n - 1, send_sem.at[k + 1])
        else:
            for copy in over:
                copy.wait_send()

    pl.when(col == lead)(lambda: body(True))
    pl.when(col != lead)(lambda: body(False))


def partner(me, step, n):
    if n & (n - 1):
        return lax.rem(me + step, n)
    other, bit = me, 1
    while bit < n:
        if step & bit:
            other = other + bit - 2 * bit * lax.rem(me // bit, 2)
        bit *= 2
    return other


def per_device(plan, matrix, diagonal, start):
    chunk, height = plan.chunk, plan.height
    n, rows, cols, phases = plan.devices, plan.rows, plan.cols, ITERS + 1
    vmem = pl.BlockSpec(memory_space=pltpu.VMEM)
    hbm = pl.BlockSpec(memory_space=pl.ANY)
    f32 = jnp.float32
    return pl.pallas_call(
        functools.partial(kernel, plan),
        out_shape=(
            jax.ShapeDtypeStruct((phases, chunk), f32),
            jax.ShapeDtypeStruct((2, ITERS), f32),
        ),
        in_specs=[hbm, hbm, hbm],
        out_specs=(vmem, vmem),
        scratch_shapes=[
            pltpu.VMEM((plan.block, cols * plan.width), f32),
            pltpu.VMEM((1, chunk), f32),
            pltpu.VMEM((1, chunk), f32),
            pltpu.VMEM((1, height, LANES), f32),
            pltpu.VMEM((cols, height, LANES), f32),
            pltpu.VMEM((phases, height, LANES), f32),
            pltpu.VMEM((n, height, LANES), f32),
            pltpu.VMEM((ITERS * rows, height, LANES), f32),
            pltpu.VMEM((phases, plan.tiles, plan.groups, LANES), f32),
            pltpu.VMEM((phases, plan.tiles, plan.groups, LANES), f32),
            pltpu.SemaphoreType.DMA,
            pltpu.SemaphoreType.DMA,
            pltpu.SemaphoreType.DMA,
            pltpu.SemaphoreType.DMA((2,)),
            pltpu.SemaphoreType.DMA((2,)),
            pltpu.SemaphoreType.DMA((phases,)),
            pltpu.SemaphoreType.DMA((phases,)),
        ],
        compiler_params=pltpu.CompilerParams(collective_id=0, has_side_effects=True),
    )(matrix, diagonal.reshape(1, chunk), start.reshape(1, chunk))


def solution(mesh):
    rows, cols = mesh.shape["row"], mesh.shape["col"]

    def run(matrix, diagonal, start):
        plan = Plan(rows, cols, matrix.shape[0], matrix.shape[1], start.shape[0])
        return per_device(plan, matrix, diagonal, start)

    in_specs = (P("row", "col"), P(("row", "col")), P(("row", "col")))
    out_specs = (P(None, ("row", "col")), P())
    return jax.shard_map(run, mesh=mesh, in_specs=in_specs, out_specs=out_specs, check_vma=False)
```

time: 31.4 us -> 28.2 us (0.90)
  Pallas kernels: 28.1 us -> 25 us
    pallas_call x1, Pallas kernels: 28.1 us -> 25 us  [per_device(): pl.pallas_call(functools.partial(kernel, plan), out_shape=(jax.ShapeDtype...]
where the time goes in v2:
time: 28.2 us; the launch traced here: 28.1 us
  Pallas kernels  25 us (89%)
  local copies, waits for them, and re-layouts  2.46 us (9%)
  between operations  0.64 us (2%)
    pallas_call x1, Pallas kernels, per_device(): pl.pallas_call(functools.partial(kernel, plan), out_shape=(jax.ShapeDtype...  25 us
    unnamed x2, local copies, waits for them, and re-layouts  2.46 us

profile of v2, /device:TPU:0, one launch (start us, length us, event | category | flops | bytes accessed | tf_op | source)
XLA Modules:
  0.0 28.1 jit_solution(1011804068754850829)
XLA Ops:
  0.6 25.0 %shard_map.50 = (f32[4,96]{1,0:T(4,128)}, f32[2,3]{1,0:T(2,128)}) custom-call(f32[192,1536]{1,0:T(8,128)} %m_hbm.1, f32[1,96]{1,0:T(1,128)} %bitcast.2, f32[1,96]{1,0:T(1,128)} %bitcast.3), custom_call_target="tpu_custom_call" | custom-call | tf_op jit(solution)/shard_map/pallas_call | solution.py:230
  25.6 1.2 %copy.7 = f32[4,96]{1,0:T(4,128)} copy(f32[4,96]{1,0:T(4,128)} %get-tuple-element.4) | data formatting | bytes 3072
  26.9 1.2 %copy.8 = f32[2,3]{1,0:T(2,128)} copy(f32[2,3]{1,0:T(2,128)} %get-tuple-element.5) | data formatting | bytes 48

commit v3 on v2

--- a/solution.py
+++ b/solution.py
@@ -230,8 +230,8 @@
     return pl.pallas_call(
         functools.partial(kernel, plan),
         out_shape=(
-            jax.ShapeDtypeStruct((phases, chunk), f32),
-            jax.ShapeDtypeStruct((2, ITERS), f32),
+            pltpu.VMEM((phases, chunk), f32),
+            pltpu.VMEM((2, ITERS), f32),
         ),
         in_specs=[hbm, hbm, hbm],
         out_specs=(vmem, vmem),

time: 28.2 us -> 26.3 us (0.933)
  local copies, waits for them, and re-layouts: 2.46 us -> 1.14 us
  Pallas kernels: 25 us -> 24.4 us
    unnamed x2, local copies, waits for them, and re-layouts: 2.46 us -> 1.14 us
    pallas_call x1, Pallas kernels: 25 us -> 24.4 us  [per_device(): pl.pallas_call(functools.partial(kernel, plan), out_shape=(pltpu.VMEM((ph...]
where the time goes in v3:
time: 26.3 us; the launch traced here: 26.2 us
  Pallas kernels  24.4 us (93%)
  local copies, waits for them, and re-layouts  1.14 us (4%)
  between operations  0.64 us (2%)
    pallas_call x1, Pallas kernels, per_device(): pl.pallas_call(functools.partial(kernel, plan), out_shape=(pltpu.VMEM((ph...  24.4 us
    unnamed x2, local copies, waits for them, and re-layouts  1.14 us

profile of v3, /device:TPU:0, one launch (start us, length us, event | category | flops | bytes accessed | tf_op | source)
XLA Modules:
  0.0 26.2 jit_solution(1651474912906003156)
XLA Ops:
  0.6 24.4 %shard_map.50 = (f32[4,96]{1,0:T(4,128)S(1)}, f32[2,3]{1,0:T(2,128)S(1)}) custom-call(f32[192,1536]{1,0:T(8,128)} %m_hbm.1, f32[1,96]{1,0:T(1,128)} %bitcast.2, f32[1,96]{1,0:T(1,128)} %bitcast.3), custom_call_target="tpu_custom_call" | custom-call | tf_op jit(solution)/shard_map/pallas_call | solution.py:230
  25.0 0.6 %copy.7 = f32[4,96]{1,0:T(4,128)} copy(f32[4,96]{1,0:T(4,128)S(1)} %get-tuple-element.2) | data formatting | bytes 3072
  25.6 0.6 %copy.8 = f32[2,3]{1,0:T(2,128)} copy(f32[2,3]{1,0:T(2,128)S(1)} %get-tuple-element.3) | data formatting | bytes 48
